TPU v7x, 32 devices: a whole 2x2x4 slice. The times are simulated.
32 devices in a mesh: lon: 8 (over y, x, core), lat: 4 (over z).
Axes of the slice: x: 2, y: 2, z: 4, core: 2. Of those that a mesh axis runs over, the one named last changes fastest.
Arguments:
- normed: bfloat16 [8, 96, 192, 192], P(None, 'lat', 'lon'), may hold values from -6 to 6
- cotangent: bfloat16 [8, 96, 192, 192], P(None, 'lat', 'lon'), may hold values from -6 to 6
- weight_qkv: bfloat16 [192, 576], replicated, may hold values from -0.4375 to 0.4375
- weight_proj: bfloat16 [192, 192], replicated, may hold values from -0.4375 to 0.4375
- bias_table: bfloat16 [64, 6, 20736], P('lat'), may hold values from -6 to 390
Outputs:
- input_grad: bfloat16 [8, 96, 192, 192], P(None, 'lat', 'lon')
- qkv_grad: float32 [192, 576], replicated
- proj_grad: float32 [192, 192], replicated
- bias_grad: float32 [64, 6, 20736], P('lat')
All inputs are finite; a program needn't handle non-finite values.
Results may differ from a plain program's by a relative error of at most 0.019.
Values may be sent and summed in bfloat16 or wider, within the bound.
No kernel may reach another device: no remote copies, remote signals or barrier semaphores. Data moves between devices by JAX's collectives and lax.ppermute only.
A program may use at most 192 MiB of HBM per device.

v0:
```python
import jax
import jax.numpy as jnp
from jax import lax
from jax.sharding import PartitionSpec as P

HEADS = 6
WIN_Z = 2
WIN_LAT = 6
WIN_LON = 12
WTOK = 144


def from_behind(block, axis, distance):
    devices = range(lax.axis_size(axis))
    route = [((i - distance) % len(devices), i) for i in devices]
    return lax.ppermute(block, axis, route)


def passed_along(block, axis, distance):
    devices = range(lax.axis_size(axis))
    route = [(i - distance, i) for i in devices if i - distance in devices]
    return lax.ppermute(block, axis, route)


def window_split(grid_field):
    levels, height, breadth = grid_field.shape[:3]
    trailing_dims = grid_field.shape[3:]
    shaped = grid_field.reshape(
        (levels // WIN_Z, WIN_Z, height // WIN_LAT, WIN_LAT, breadth // WIN_LON, WIN_LON)
        + trailing_dims
    )
    axes_order = (0, 2, 4, 1, 3, 5) + tuple(range(6, 6 + len(trailing_dims)))
    return shaped.transpose(axes_order).reshape((-1, WTOK) + trailing_dims)


def window_merge(windowed, levels, height, breadth):
    channels = windowed.shape[-1]
    shaped = windowed.reshape(
        levels // WIN_Z, height // WIN_LAT, breadth // WIN_LON, WIN_Z, WIN_LAT, WIN_LON, channels
    )
    return shaped.transpose(0, 3, 1, 4, 2, 5, 6).reshape(levels, height, breadth, channels)


def window_backward(
    block_in, block_cot, block_region, block_live, block_types, bias_rows, weight_qkv, weight_proj
):
    windows = block_in.shape[0]
    channels = block_in.shape[2]
    head_dim = channels // HEADS
    softmax_scale = head_dim ** (-0.5)
    high = lax.Precision.HIGHEST
    f32 = jnp.float32
    projected = jnp.einsum("bnc,cf->bnf", block_in, weight_qkv, preferred_element_type=f32).astype(
        jnp.bfloat16
    )
    projected = projected.reshape(windows, WTOK, 3, HEADS, head_dim)
    queries = projected[:, :, 0]
    key_rows = projected[:, :, 1]
    values = projected[:, :, 2]
    bias_add = jnp.dot(
        block_types.astype(jnp.bfloat16), bias_rows, preferred_element_type=f32
    ).reshape(windows, HEADS, WTOK, WTOK)
    scores = (
        jnp.einsum("bqhd,bkhd->bhqk", queries, key_rows, preferred_element_type=f32) * softmax_scale
        + bias_add
    )
    allowed = (block_region[:, :, None] == block_region[:, None, :]) & (
        block_live[:, :, None] == block_live[:, None, :]
    )
    allowed = allowed[:, None]
    peak_score = jnp.max(jnp.where(allowed, scores, -1e30), axis=-1, keepdims=True)
    exp_terms = jnp.where(allowed, jnp.exp(scores - peak_score), 0.0)
    attn_probs = exp_terms / jnp.sum(exp_terms, axis=-1, keepdims=True)
    probs_b = attn_probs.astype(jnp.bfloat16)
    mixed = jnp.einsum("bhqk,bkhd->bqhd", probs_b, values, preferred_element_type=f32).astype(
        jnp.bfloat16
    )
    mixed = mixed.reshape(windows, WTOK, channels)
    grad_proj = jnp.einsum("bnc,bnf->cf", mixed, block_cot, preferred_element_type=f32)
    mixed_grad = jnp.einsum(
        "bnf,cf->bnc", block_cot, weight_proj, preferred_element_type=f32
    ).astype(jnp.bfloat16)
    mixed_grad = mixed_grad.reshape(windows, WTOK, HEADS, head_dim)
    prob_grad = jnp.einsum("bqhd,bkhd->bhqk", mixed_grad, values, preferred_element_type=f32)
    row_delta = jnp.sum(attn_probs * prob_grad, axis=-1, keepdims=True)
    score_grad = attn_probs * (prob_grad - row_delta)
    grad_bias = jnp.dot(
        block_types.T, score_grad.reshape(windows, -1), precision=high, preferred_element_type=f32
    )
    score_grad_b = score_grad.astype(jnp.bfloat16)
    query_grad = (
        jnp.einsum("bhqk,bkhd->bqhd", score_grad_b, key_rows, preferred_element_type=f32)
        * softmax_scale
    ).astype(jnp.bfloat16)
    key_grad = (
        jnp.einsum("bhqk,bqhd->bkhd", score_grad_b, queries, preferred_element_type=f32)
        * softmax_scale
    ).astype(jnp.bfloat16)
    value_grad = jnp.einsum(
        "bhqk,bqhd->bkhd", probs_b, mixed_grad, preferred_element_type=f32
    ).astype(jnp.bfloat16)
    cols_grad = jnp.stack([query_grad, key_grad, value_grad], axis=2).reshape(
        windows, WTOK, 3 * channels
    )
    grad_qkv = jnp.einsum("bnc,bnf->cf", block_in, cols_grad, preferred_element_type=f32)
    grad_in = jnp.einsum("bnf,cf->bnc", cols_grad, weight_qkv, preferred_element_type=f32).astype(
        jnp.bfloat16
    )
    return (grad_in, grad_qkv, grad_proj, grad_bias)


def local(normed, cotangent, weight_qkv, weight_proj, bias_table):
    levels, height, breadth, channels = normed.shape
    level_shift = WIN_Z // 2
    lat_shift = WIN_LAT // 2
    lon_shift = WIN_LON // 2
    normed = jnp.roll(normed, -level_shift, axis=0)
    cotangent = jnp.roll(cotangent, -level_shift, axis=0)
    across = from_behind((normed[:, :, :lon_shift], cotangent[:, :, :lon_shift]), "lon", -1)
    wide_in = jnp.concatenate([normed[:, :, lon_shift:], across[0]], axis=2)
    wide_cot = jnp.concatenate([cotangent[:, :, lon_shift:], across[1]], axis=2)
    upward = passed_along((wide_in[:, :lat_shift], wide_cot[:, :lat_shift]), "lat", -1)
    frame_in = jnp.concatenate([wide_in[:, lat_shift:], upward[0]], axis=1)
    frame_cot = jnp.concatenate([wide_cot[:, lat_shift:], upward[1]], axis=1)
    is_last = lax.axis_index("lat") == lax.axis_size("lat") - 1
    row_index = jnp.arange(height, dtype=jnp.int32)
    live_rows = jnp.logical_not(is_last & (row_index >= height - lat_shift))
    live_field = jnp.broadcast_to(live_rows[None, :, None], (levels, height, breadth))
    level_index = jnp.arange(levels, dtype=jnp.int32)
    wrapped_levels = (level_index >= levels - level_shift).astype(jnp.int32)
    wrapped_field = jnp.broadcast_to(wrapped_levels[:, None, None], (levels, height, breadth))
    level_windows = levels // WIN_Z
    lat_windows = height // WIN_LAT
    lon_windows = breadth // WIN_LON
    types_local = level_windows * lat_windows
    level_part = jnp.arange(level_windows, dtype=jnp.int32)[:, None, None]
    lat_part = jnp.arange(lat_windows, dtype=jnp.int32)[None, :, None]
    kinds = jnp.broadcast_to(
        lat_part * level_windows + level_part, (level_windows, lat_windows, lon_windows)
    )
    onehot = (
        kinds.reshape(-1)[:, None] == jnp.arange(types_local, dtype=jnp.int32)[None, :]
    ).astype(jnp.float32)
    bias_rows = bias_table.reshape(types_local, -1)
    framed_in = window_split(frame_in)
    window_total = framed_in.shape[0]
    block_size = max((divisor for divisor in range(1, 17) if window_total % divisor == 0))
    blocks = window_total // block_size

    def regroup(array):
        return array.reshape((blocks, block_size) + array.shape[1:])

    def step_block(totals, pieces):
        grad_in, grad_qkv, grad_proj, grad_bias = window_backward(
            pieces[0],
            pieces[1],
            pieces[2],
            pieces[3],
            pieces[4],
            bias_rows,
            weight_qkv,
            weight_proj,
        )
        return ((totals[0] + grad_qkv, totals[1] + grad_proj, totals[2] + grad_bias), grad_in)

    start = (
        jnp.zeros((channels, 3 * channels), jnp.float32),
        jnp.zeros((channels, channels), jnp.float32),
        jnp.zeros((types_local, HEADS * WTOK * WTOK), jnp.float32),
    )
    pieces = (
        regroup(framed_in),
        regroup(window_split(frame_cot)),
        regroup(window_split(wrapped_field)),
        regroup(window_split(live_field)),
        regroup(onehot),
    )
    totals, grads = lax.scan(step_block, start, pieces)
    framed_grad = window_merge(grads.reshape(window_total, WTOK, channels), levels, height, breadth)
    returned = passed_along(framed_grad[:, height - lat_shift :], "lat", 1)
    wide_grad = jnp.concatenate([returned, framed_grad[:, : height - lat_shift]], axis=1)
    sideways = from_behind(wide_grad[:, :, breadth - lon_shift :], "lon", 1)
    shifted_grad = jnp.concatenate([sideways, wide_grad[:, :, : breadth - lon_shift]], axis=2)
    input_grad = jnp.roll(shifted_grad, level_shift, axis=0)
    lat_qkv, lat_proj = (
        lax.psum(totals[0].astype(jnp.bfloat16), "lat").astype(jnp.float32),
        lax.psum(totals[1].astype(jnp.bfloat16), "lat").astype(jnp.float32),
    )
    bias_grad, qkv_grad, proj_grad = (
        lax.psum(totals[2].astype(jnp.bfloat16), "lon").astype(jnp.float32),
        lax.psum(lat_qkv.astype(jnp.bfloat16), "lon").astype(jnp.float32),
        lax.psum(lat_proj.astype(jnp.bfloat16), "lon").astype(jnp.float32),
    )
    return (input_grad, qkv_grad, proj_grad, bias_grad.reshape(types_local, HEADS, WTOK * WTOK))


def solution(mesh):
    in_specs = (
        P(None, "lat", "lon", None),
        P(None, "lat", "lon", None),
        P(),
        P(),
        P("lat", None, None),
    )
    out_specs = (P(None, "lat", "lon", None), P(), P(), P("lat", None, None))
    return jax.shard_map(local, mesh=mesh, in_specs=in_specs, out_specs=out_specs, check_vma=False)
```

profile of v0, /device:TPU:0, one launch (start us, length us, event | category | flops | bytes accessed | tf_op | source)
XLA Modules:
  0.0 629.4 jit_solution(3365991301374217343)
XLA Ops:
  10.1 3.4 collective-permute-start
  18.0 1.7 slice.91
  25.9 4.3 copy.139
  36.0 1.8 slice_maximum_fusion.1
  37.8 3.2 slice_maximum_fusion
  40.9 2.2 collective-permute-done.1
  45.7 2.6 reshape.113
  48.3 2.4 copy.126
  50.6 2.6 reshape.129
  54.4 2.6 pad_maximum_fusion.6
  58.3 2.6 reshape.115
  60.9 4.0 copy.127
  64.9 4.0 reshape.130
  68.9 396.9 %while.17 = (s32[]{:T(128)}, f32[192,576]{1,0:T(8,128)}, f32[192,192]{1,0:T(8,128)}, f32[16,124416]{1,0:T(8,128)}, bf16[2,16,144,192]{3,1,0,2:T(8,128)(2,1)}, /*...) while((s32[]{:T(128)}, f32[192,576]{1,0:T(8,128)}, ...), condition=%wide.region_4.5_spmd.clone, body=%wide.region_0.4_spmd.clone.sunk | while | flops 3127491072 | bytes 382142976 | solution.py:178
  72.4 15.1 %dot_general.59 = bf16[6,144,144,16]{2,1,0,3:T(8,128)(2,1)} reshape(bf16[124416,16]{0,1:T(8,128)(2,1)} %bitcast.192) | data formatting | bytes 7962624 | tf_op jit(solution)/shard_map/while/body/eval_jaxpr/dot_general | solution.py:60
  87.5 12.4 %fusion.128 = f32[16,6,144,144]{3,0,2,1:T(8,128)} fusion(bf16[6,144,144,16]{2,1,0,3:T(8,128)(2,1)} %dot_general.59, f32[2,16,16]{2,1,0:T(8,128)S(1)} %get-tuple-element.332, s32[]{:T(128)S(6)} %copy.169), kind=kOutput, calls=%fused_computation.8.clone.1 | convolution fusion | flops 63700992 | bytes 11948036 | tf_op jit(solution)/shard_map/while/body/eval_jaxpr/dot_general | solution.py:60
  99.8 17.0 %copy.157 = f32[16,6,144,144]{2,3,1,0:T(8,128)} copy(f32[16,6,144,144]{3,0,2,1:T(8,128)} %fusion.128) | data formatting | bytes 15925248 | tf_op jit(solution)/shard_map/while/body/eval_jaxpr/dot_general | solution.py:60
  116.9 2.3 convolution_convert_fusion.6
  119.2 5.1 copy.158
  124.3 13.1 %multiply_add_fusion.2 = f32[16,6,144,144]{2,3,1,0:T(8,128)} fusion(f32[16,6,144,144]{2,3,1,0:T(8,128)} %copy.157, bf16[16,144,3,6,32]{1,4,3,2,0:T(8,128)(2,1)} %bitcast.182), kind=kOutput, calls=%fused_computation.7.clone.1 | convolution fusion | flops 131383296 | bytes 25264128 | tf_op jit(solution)/shard_map/while/body/eval_jaxpr/bqhd,bkhd->bhqk/dot_general | solution.py:64
  138.5 15.3 %fusion.129 = (f32[16,6,144]{2,1,0:T(8,128)S(1)}, f32[16,6,144,144]{2,3,1,0:T(8,128)}) fusion(f32[16,6,144,144]{2,3,1,0:T(8,128)} %multiply_add_fusion.2, pred[16,144,144]{1,2,0:T(8,128)(4,1)S(1)} %compare_and_fusion.2), kind=kOutput, calls=%fused_computation.93.clone.1 | output fusion | flops 7962767 | bytes 16312320 | tf_op jit(solution)/shard_map/while/body/eval_jaxpr/sub | solution.py:72
  153.8 8.0 %fusion.130 = bf16[16,144,1,6,32]{1,4,3,0,2:T(8,128)(2,1)S(1)} fusion(bf16[16,144,6,32]{1,3,2,0:T(8,128)(2,1)} %bitcast.193, f32[16,6,144,144]{2,3,1,0:T(8,128)} %get-tuple-element.289, f32[16,6,144]{2,1,0:T(8,128)S(1)} %get-tuple-element.290), kind=kOutput, calls=%fused_computation.33.clone.1 | convolution fusion | flops 131825664 | bytes 9787392 | tf_op jit(solution)/shard_map/while/body/eval_jaxpr/bhqk,bqhd->bkhd/dot_general | solution.py:99
  163.4 9.7 %multiply_reduce_fusion.2 = (f32[16,6,144]{2,1,0:T(8,128)S(1)}, f32[16,6,144,144]{2,3,1,0:T(8,128)}) fusion(f32[16,6,144,144]{2,3,1,0:T(8,128)S(1)} %copy-done.1, f32[16,6,144]{2,1,0:T(8,128)S(1)} %get-tuple-element.290, bf16[16,144,6,32]{1,3,2,0:T(8,128)(2,1)} %bitcast.194, bf16[16,144,3,6,32]{1,4,3,2,0:T(8,128)(2,1)} %bitcast.183), kind=kOutput, calls=%fused_computation.3.clone.1 | convolution fusion | flops 133360128 | bytes 19181568 | tf_op jit(solution)/shard_map/while/body/eval_jaxpr/bqhd,bkhd->bhqk/dot_general | solution.py:84
  173.1 10.1 %subtract_multiply_fusion.2 = f32[16,6,144,144]{2,3,1,0:T(8,128)S(1)} fusion(f32[16,6,144,144]{2,3,1,0:T(8,128)} %get-tuple-element.291, f32[16,6,144]{2,1,0:T(8,128)S(1)} %get-tuple-element.292, f32[16,6,144,144]{2,3,1,0:T(8,128)} %get-tuple-element.289, f32[16,6,144]{2,1,0:T(8,128)S(1)} %get-tuple-element.290), kind=kLoop, calls=%fused_computation.2.clone.1 | loop fusion | flops 5971968 | bytes 23998464 | tf_op jit(solution)/shard_map/while/body/eval_jaxpr/mul | solution.py:86
  183.2 5.0 fusion.131
  188.4 2.6 fusion.132
  192.4 2.8 copy.159
  195.2 4.5 fusion.133
  199.7 6.8 %fusion.134 = bf16[16,6,32,144]{3,2,1,0:T(8,128)(2,1)S(1)} fusion(bf16[16,144,3,6,32]{1,4,3,2,0:T(8,128)(2,1)} %bitcast.186, f32[16,6,144,144]{2,3,1,0:T(8,128)} %get-tuple-element.289, f32[16,6,144]{2,1,0:T(8,128)S(1)} %copy-done.8), kind=kOutput, calls=%fused_computation.27.clone.1 | convolution fusion | flops 131825664 | bytes 16668672 | tf_op jit(solution)/shard_map/while/body/eval_jaxpr/bhqk,bkhd->bqhd/dot_general | solution.py:75
  207.2 17.1 %copy.160 = f32[16,6,144,144]{3,2,1,0:T(8,128)} copy(f32[16,6,144,144]{2,3,1,0:T(8,128)} %copy-done) | data formatting | bytes 15925248 | tf_op jit(solution)/shard_map/while/body/eval_jaxpr/mul | solution.py:86
  224.3 23.2 %reshape.132 = f32[16,124416]{1,0:T(8,128)} reshape(f32[16,6,144,144]{3,2,1,0:T(8,128)} %copy.160) | data formatting | bytes 15925248 | tf_op jit(solution)/shard_map/while/body/eval_jaxpr/reshape | solution.py:88
  247.5 11.2 %convolution_add_fusion.2 = f32[16,124416]{1,0:T(8,128)} fusion(f32[16,124416]{1,0:T(8,128)} %reshape.132, f32[16,124416]{1,0:T(8,128)} %get-tuple-element.311, pred[]{:T(512)S(6)} %compare.3, f32[2,16,16]{2,1,0:T(8,128)S(1)} %get-tuple-element.332, s32[]{:T(128)S(6)} %copy.169), kind=kOutput, calls=%fused_computation.1.clone.1 | convolution fusion | flops 386187264 | bytes 23896068 | tf_op jit(solution)/shard_map/while/body/eval_jaxpr/dot_general | solution.py:87
  265.9 15.1 %dot_general.59 = bf16[6,144,144,16]{2,1,0,3:T(8,128)(2,1)} reshape(bf16[124416,16]{0,1:T(8,128)(2,1)} %bitcast.192) | data formatting | bytes 7962624 | tf_op jit(solution)/shard_map/while/body/eval_jaxpr/dot_general | solution.py:60
  281.0 12.4 %fusion.128 = f32[16,6,144,144]{3,0,2,1:T(8,128)} fusion(bf16[6,144,144,16]{2,1,0,3:T(8,128)(2,1)} %dot_general.59, f32[2,16,16]{2,1,0:T(8,128)S(1)} %get-tuple-element.332, s32[]{:T(128)S(6)} %copy.169), kind=kOutput, calls=%fused_computation.8.clone.1 | convolution fusion | flops 63700992 | bytes 11948036 | tf_op jit(solution)/shard_map/while/body/eval_jaxpr/dot_general | solution.py:60
  293.4 17.0 %copy.157 = f32[16,6,144,144]{2,3,1,0:T(8,128)} copy(f32[16,6,144,144]{3,0,2,1:T(8,128)} %fusion.128) | data formatting | bytes 15925248 | tf_op jit(solution)/shard_map/while/body/eval_jaxpr/dot_general | solution.py:60
  310.4 2.3 convolution_convert_fusion.6
  312.7 4.8 copy.158
  317.6 13.1 %multiply_add_fusion.2 = f32[16,6,144,144]{2,3,1,0:T(8,128)} fusion(f32[16,6,144,144]{2,3,1,0:T(8,128)} %copy.157, bf16[16,144,3,6,32]{1,4,3,2,0:T(8,128)(2,1)} %bitcast.182), kind=kOutput, calls=%fused_computation.7.clone.1 | convolution fusion | flops 131383296 | bytes 25264128 | tf_op jit(solution)/shard_map/while/body/eval_jaxpr/bqhd,bkhd->bhqk/dot_general | solution.py:64
  331.7 15.3 %fusion.129 = (f32[16,6,144]{2,1,0:T(8,128)S(1)}, f32[16,6,144,144]{2,3,1,0:T(8,128)}) fusion(f32[16,6,144,144]{2,3,1,0:T(8,128)} %multiply_add_fusion.2, pred[16,144,144]{1,2,0:T(8,128)(4,1)S(1)} %compare_and_fusion.2), kind=kOutput, calls=%fused_computation.93.clone.1 | output fusion | flops 7962767 | bytes 16312320 | tf_op jit(solution)/shard_map/while/body/eval_jaxpr/sub | solution.py:72
  347.1 8.0 %fusion.130 = bf16[16,144,1,6,32]{1,4,3,0,2:T(8,128)(2,1)S(1)} fusion(bf16[16,144,6,32]{1,3,2,0:T(8,128)(2,1)} %bitcast.193, f32[16,6,144,144]{2,3,1,0:T(8,128)} %get-tuple-element.289, f32[16,6,144]{2,1,0:T(8,128)S(1)} %get-tuple-element.290), kind=kOutput, calls=%fused_computation.33.clone.1 | convolution fusion | flops 131825664 | bytes 9787392 | tf_op jit(solution)/shard_map/while/body/eval_jaxpr/bhqk,bqhd->bkhd/dot_general | solution.py:99
  356.7 9.7 %multiply_reduce_fusion.2 = (f32[16,6,144]{2,1,0:T(8,128)S(1)}, f32[16,6,144,144]{2,3,1,0:T(8,128)}) fusion(f32[16,6,144,144]{2,3,1,0:T(8,128)S(1)} %copy-done.1, f32[16,6,144]{2,1,0:T(8,128)S(1)} %get-tuple-element.290, bf16[16,144,6,32]{1,3,2,0:T(8,128)(2,1)} %bitcast.194, bf16[16,144,3,6,32]{1,4,3,2,0:T(8,128)(2,1)} %bitcast.183), kind=kOutput, calls=%fused_computation.3.clone.1 | convolution fusion | flops 133360128 | bytes 19181568 | tf_op jit(solution)/shard_map/while/body/eval_jaxpr/bqhd,bkhd->bhqk/dot_general | solution.py:84
  366.3 10.1 %subtract_multiply_fusion.2 = f32[16,6,144,144]{2,3,1,0:T(8,128)S(1)} fusion(f32[16,6,144,144]{2,3,1,0:T(8,128)} %get-tuple-element.291, f32[16,6,144]{2,1,0:T(8,128)S(1)} %get-tuple-element.292, f32[16,6,144,144]{2,3,1,0:T(8,128)} %get-tuple-element.289, f32[16,6,144]{2,1,0:T(8,128)S(1)} %get-tuple-element.290), kind=kLoop, calls=%fused_computation.2.clone.1 | loop fusion | flops 5971968 | bytes 23998464 | tf_op jit(solution)/shard_map/while/body/eval_jaxpr/mul | solution.py:86
  376.5 5.0 fusion.131
  381.7 2.6 fusion.132
  385.7 2.8 copy.159
  388.5 4.5 fusion.133
  393.1 6.8 %fusion.134 = bf16[16,6,32,144]{3,2,1,0:T(8,128)(2,1)S(1)} fusion(bf16[16,144,3,6,32]{1,4,3,2,0:T(8,128)(2,1)} %bitcast.186, f32[16,6,144,144]{2,3,1,0:T(8,128)} %get-tuple-element.289, f32[16,6,144]{2,1,0:T(8,128)S(1)} %copy-done.8), kind=kOutput, calls=%fused_computation.27.clone.1 | convolution fusion | flops 131825664 | bytes 16668672 | tf_op jit(solution)/shard_map/while/body/eval_jaxpr/bhqk,bkhd->bqhd/dot_general | solution.py:75
  400.5 17.1 %copy.160 = f32[16,6,144,144]{3,2,1,0:T(8,128)} copy(f32[16,6,144,144]{2,3,1,0:T(8,128)} %copy-done) | data formatting | bytes 15925248 | tf_op jit(solution)/shard_map/while/body/eval_jaxpr/mul | solution.py:86
  417.6 23.2 %reshape.132 = f32[16,124416]{1,0:T(8,128)} reshape(f32[16,6,144,144]{3,2,1,0:T(8,128)} %copy.160) | data formatting | bytes 15925248 | tf_op jit(solution)/shard_map/while/body/eval_jaxpr/reshape | solution.py:88
  440.8 13.3 %convolution_add_fusion.2 = f32[16,124416]{1,0:T(8,128)} fusion(f32[16,124416]{1,0:T(8,128)} %reshape.132, f32[16,124416]{1,0:T(8,128)} %get-tuple-element.311, pred[]{:T(512)S(6)} %compare.3, f32[2,16,16]{2,1,0:T(8,128)S(1)} %get-tuple-element.332, s32[]{:T(128)S(6)} %copy.169), kind=kOutput, calls=%fused_computation.1.clone.1 | convolution fusion | flops 386187264 | bytes 23896068 | tf_op jit(solution)/shard_map/while/body/eval_jaxpr/dot_general | solution.py:87
  465.8 1.8 convert_element_type.78
  469.2 5.5 convert_element_type.82
  474.8 9.0 %reshape.117 = bf16[16,6,20736]{2,1,0:T(8,128)(2,1)} reshape(bf16[16,124416]{1,0:T(8,128)(2,1)} %convert_element_type.82) | data formatting | bytes 7962624 | tf_op jit(solution)/shard_map/reshape | solution.py:194
  483.8 21.9 %all-reduce.7.cloned.1.call-done = (bf16[192,576]{1,0:T(8,128)(2,1)}, bf16[192,192]{1,0:T(8,128)(2,1)}) async-done(((bf16[192,576]{1,0:T(8,128)(2,1)}, bf16[192,192]{1,0:T(8,128)(2,1)}), (bf16[192,576]{1,0:T(8,128)(2,1)}, bf16[192,192]{1,0:T(8,128)(2,1)})) %all-reduce.7.cloned.1.call-update) | async-done | bytes 294928 | tf_op jit(solution)/shard_map/psum | solution.py:186
  505.7 4.9 reshape_reshape.19
  510.6 3.9 copy.115
  514.5 5.2 reshape.116
  519.7 3.6 collective-permute-start.4
  523.5 4.5 collective-permute-done.4
  528.2 19.4 %collective-permute-done.5 = bf16[8,24,6,192]{3,0,2,1:T(8,128)(2,1)S(1)} collective-permute-done((bf16[8,24,6,192]{3,0,2,1:T(8,128)(2,1)S(1)}, bf16[8,24,6,192]{3,0,2,1:T(8,128)(2,1)S(1)}, u32[]{:S(2)}, u32[]{:S(2)}) %collective-permute-start.5) | collective-permute-done | bytes 442400 | tf_op jit(solution)/shard_map/ppermute | solution.py:16
  548.9 1.9 copy.116
  550.8 61.7 %all-reduce.5.cloned.1.call-done = (bf16[16,6,20736]{2,1,0:T(8,128)(2,1)}, bf16[192,576]{1,0:T(8,128)(2,1)}, bf16[192,192]{1,0:T(8,128)(2,1)}) async-done(((bf16[16,6,20736]{2,1,0:T(8,128)(2,1)}, bf16[192,576]{1,0:T(8,128)(2,1)}, bf16[192,192]{1,0:T(8,128)(2,1)}), (bf16[16,6,20736]{2,1,0:T(8,128)(2,1)}, bf16[192,576]{1,0:T(8,128)(2,1)}, bf16[192,192]{1,0:T(8,128)(2,1)})) %all-reduce.5.cloned.1.call-update) | async-done | bytes 4276240 | tf_op jit(solution)/shard_map/psum | solution.py:190
  612.4 1.8 convert_element_type.79
  615.8 6.5 %copy.117 = f32[16,6,20736]{2,0,1:T(8,128)} copy(bf16[16,6,20736]{2,1,0:T(8,128)(2,1)} %get-tuple-element.197) | data formatting | bytes 11943936
  (160 shorter events, 52.0 us)
Async XLA Ops:
  7.2 1.6 slice-start.2
  7.2 498.5 %all-reduce.7.cloned.1.call-start = ((), (), s32[]{:S(2)}) async-start(), calls=%async_computation.1 | async-start | bytes 688128 | tf_op jit(solution)/shard_map/psum | solution.py:186
  7.2 2.0 slice-start.3
  9.2 4.3 copy-start.9
  9.3 4.2 slice-start.4
  10.1 20.1 %collective-permute-start = (bf16[8,24,6,192]{3,1,2,0:T(8,128)(2,1)}, bf16[8,24,6,192]{3,1,2,0:T(8,128)(2,1)}, u32[]{:S(2)}, u32[]{:S(2)}) collective-permute-start(bf16[8,24,6,192]{3,1,2,0:T(8,128)(2,1)} %slice.92), channel_id=1, source_target_pairs={{4,0},{8,4},{12,8},{16,12},{20,16},{24,20},{28,24},{0,28},{5,1},{9... | collective-permute-start | bytes 1327112 | tf_op jit(solution)/shard_map/ppermute | solution.py:16
  13.5 1.0 slice-start.5
  14.5 1.4 copy-start.10
  16.8 15.9 %collective-permute-start.2 = (bf16[8,24,6,192]{3,1,2,0:T(8,128)(2,1)}, bf16[8,24,6,192]{3,1,2,0:T(8,128)(2,1)}, u32[]{:S(2)}, u32[]{:S(2)}) collective-permute-start(bf16[8,24,6,192]{3,1,2,0:T(8,128)(2,1)} %slice.96), channel_id=1, source_target_pairs={{4,0},{8,4},{12,8},{16,12},{20,16},{24,20},{28,24},{0,28},{5,1},{9... | collective-permute-start | bytes 1327112 | tf_op jit(solution)/shard_map/ppermute | solution.py:16
  18.0 2.2 copy-start.11
  25.9 4.3 copy-start.20
  31.4 11.8 %collective-permute-start.1 = (bf16[8,3,24,192]{3,2,1,0:T(8,128)(2,1)S(1)}, bf16[8,3,24,192]{3,2,1,0:T(8,128)(2,1)S(1)}, u32[]{:S(2)}, u32[]{:S(2)}) collective-permute-start(bf16[8,3,24,192]{3,2,1,0:T(8,128)(2,1)S(1)} %copy.101), channel_id=1, source_target_pairs={{1,0},{2,1},{3,2},{5,4},{6,5},{7,6},{9,8},{10,9},{11,10},{13,12},{... | collective-permute-start | bytes 663560 | tf_op jit(solution)/shard_map/ppermute | solution.py:22
  34.5 18.7 %collective-permute-start.3 = (bf16[8,3,24,192]{3,2,1,0:T(8,128)(2,1)}, bf16[8,3,24,192]{3,2,1,0:T(8,128)(2,1)}, u32[]{:S(2)}, u32[]{:S(2)}) collective-permute-start(bf16[8,3,24,192]{3,2,1,0:T(8,128)(2,1)} %copy.108), channel_id=1, source_target_pairs={{1,0},{2,1},{3,2},{5,4},{6,5},{7,6},{9,8},{10,9},{11,10},{13,12},{... | collective-permute-start | bytes 663560 | tf_op jit(solution)/shard_map/ppermute | solution.py:22
  69.2 18.3 %copy-start.3 = (bf16[2,16,144,192]{3,2,1,0:T(8,128)(2,1)}, bf16[2,16,144,192]{3,2,1,0:T(8,128)(2,1)S(1)}, u32[]{:S(2)}) copy-start(bf16[2,16,144,192]{3,2,1,0:T(8,128)(2,1)S(1)} %get-tuple-element.334) | copy-start | bytes 5308420 | tf_op jit(solution)/shard_map/while
  99.8 17.0 %copy-start.5 = (bf16[192,576]{1,0:T(8,128)(2,1)S(1)}, bf16[192,576]{1,0:T(8,128)(2,1)}, u32[]{:S(2)}) copy-start(bf16[192,576]{1,0:T(8,128)(2,1)} %get-tuple-element.329) | copy-start | bytes 663556 | tf_op jit(solution)/shard_map/while
  124.3 13.2 %copy-start.16 = (s32[2,16,144]{2,1,0:T(8,128)S(1)}, s32[2,16,144]{2,1,0:T(8,128)}, u32[]{:S(2)}) copy-start(s32[2,16,144]{2,1,0:T(8,128)} %get-tuple-element.330) | copy-start | bytes 55300 | tf_op jit(solution)/shard_map/while
  124.3 13.1 %copy-start.19 = (pred[2,16,144]{2,1,0:T(8,128)(4,1)S(1)}, pred[2,16,144]{2,1,0:T(8,128)(4,1)}, u32[]{:S(2)}) copy-start(pred[2,16,144]{2,1,0:T(8,128)(4,1)} %get-tuple-element.331) | copy-start | bytes 13828 | tf_op jit(solution)/shard_map/while
  153.8 19.3 %copy-start.7 = (f32[16,6,144]{2,1,0:T(8,128)}, f32[16,6,144]{2,1,0:T(8,128)S(1)}, u32[]{:S(2)}) copy-start(f32[16,6,144]{2,1,0:T(8,128)S(1)} %get-tuple-element.290) | copy-start | bytes 165892 | tf_op jit(solution)/shard_map/while
  153.8 9.6 %copy-start.1 = (f32[16,6,144,144]{2,3,1,0:T(8,128)S(1)}, f32[16,6,144,144]{2,3,1,0:T(8,128)}, u32[]{:S(2)}) copy-start(f32[16,6,144,144]{2,3,1,0:T(8,128)} %get-tuple-element.289) | copy-start | bytes 23887876 | tf_op jit(solution)/shard_map/while
  183.2 5.3 copy-start
  192.4 2.8 copy-start.2
  192.4 2.8 copy-start.14
  195.2 4.5 copy-start.8
  199.7 6.8 %copy-start.15 = (f32[192,576]{1,0:T(8,128)}, f32[192,576]{1,0:T(8,128)S(1)}, u32[]{:S(2)}) copy-start(f32[192,576]{1,0:T(8,128)S(1)} %fusion.133) | copy-start | bytes 1327108 | tf_op jit(solution)/shard_map/while
  199.7 6.8 %copy-start.4 = (bf16[2,16,144,192]{3,2,1,0:T(8,128)(2,1)S(1)}, bf16[2,16,144,192]{3,2,1,0:T(8,128)(2,1)}, u32[]{:S(2)}) copy-start(bf16[2,16,144,192]{3,2,1,0:T(8,128)(2,1)} %copy-done.3) | copy-start | bytes 5308420 | tf_op jit(solution)/shard_map/while
  199.7 6.8 %copy-start.17 = (f32[192,192]{1,0:T(8,128)S(1)}, f32[192,192]{1,0:T(8,128)}, u32[]{:S(2)}) copy-start(f32[192,192]{1,0:T(8,128)} %get-tuple-element.310) | copy-start | bytes 442372 | tf_op jit(solution)/shard_map/while
  207.2 17.1 %copy-start.18 = (f32[192,192]{1,0:T(8,128)}, f32[192,192]{1,0:T(8,128)S(1)}, u32[]{:S(2)}) copy-start(f32[192,192]{1,0:T(8,128)S(1)} %fusion.135) | copy-start | bytes 442372 | tf_op jit(solution)/shard_map/while
  224.3 34.4 %slice-start = ((s8[4718592]{0:T(1024)(128)(4,1)}), s8[524288]{0:T(1024)(128)(4,1)S(1)}, s32[]{:S(2)}) async-start(s8[4718592]{0:T(1024)(128)(4,1)} %bitcast.188), calls=%async_computation.2 | async-start | bytes 1048576 | tf_op jit(solution)/shard_map/while
  247.5 11.2 %slice-start.1 = ((s8[4718592]{0:T(1024)(128)(4,1)}), s8[4194304]{0:T(1024)(128)(4,1)S(1)}, s32[]{:S(2)}) async-start(s8[4718592]{0:T(1024)(128)(4,1)} %bitcast.188), calls=%async_computation.3 | async-start | bytes 8388608 | tf_op jit(solution)/shard_map/while
  247.5 11.2 %copy-start.6 = (bf16[192,576]{1,0:T(8,128)(2,1)S(1)}, bf16[192,576]{1,0:T(8,128)(2,1)}, u32[]{:S(2)}) copy-start(bf16[192,576]{1,0:T(8,128)(2,1)} %get-tuple-element.329) | copy-start | bytes 663556 | tf_op jit(solution)/shard_map/while
  258.7 1.7 copy-start.12
  260.9 1.4 copy-start.13
  262.7 18.3 %copy-start.3 = (bf16[2,16,144,192]{3,2,1,0:T(8,128)(2,1)}, bf16[2,16,144,192]{3,2,1,0:T(8,128)(2,1)S(1)}, u32[]{:S(2)}) copy-start(bf16[2,16,144,192]{3,2,1,0:T(8,128)(2,1)S(1)} %get-tuple-element.334) | copy-start | bytes 5308420 | tf_op jit(solution)/shard_map/while
  293.4 17.0 %copy-start.5 = (bf16[192,576]{1,0:T(8,128)(2,1)S(1)}, bf16[192,576]{1,0:T(8,128)(2,1)}, u32[]{:S(2)}) copy-start(bf16[192,576]{1,0:T(8,128)(2,1)} %get-tuple-element.329) | copy-start | bytes 663556 | tf_op jit(solution)/shard_map/while
  317.6 13.1 %copy-start.16 = (s32[2,16,144]{2,1,0:T(8,128)S(1)}, s32[2,16,144]{2,1,0:T(8,128)}, u32[]{:S(2)}) copy-start(s32[2,16,144]{2,1,0:T(8,128)} %get-tuple-element.330) | copy-start | bytes 55300 | tf_op jit(solution)/shard_map/while
  317.6 13.1 %copy-start.19 = (pred[2,16,144]{2,1,0:T(8,128)(4,1)S(1)}, pred[2,16,144]{2,1,0:T(8,128)(4,1)}, u32[]{:S(2)}) copy-start(pred[2,16,144]{2,1,0:T(8,128)(4,1)} %get-tuple-element.331) | copy-start | bytes 13828 | tf_op jit(solution)/shard_map/while
  347.1 19.3 %copy-start.7 = (f32[16,6,144]{2,1,0:T(8,128)}, f32[16,6,144]{2,1,0:T(8,128)S(1)}, u32[]{:S(2)}) copy-start(f32[16,6,144]{2,1,0:T(8,128)S(1)} %get-tuple-element.290) | copy-start | bytes 165892 | tf_op jit(solution)/shard_map/while
  347.1 9.6 %copy-start.1 = (f32[16,6,144,144]{2,3,1,0:T(8,128)S(1)}, f32[16,6,144,144]{2,3,1,0:T(8,128)}, u32[]{:S(2)}) copy-start(f32[16,6,144,144]{2,3,1,0:T(8,128)} %get-tuple-element.289) | copy-start | bytes 23887876 | tf_op jit(solution)/shard_map/while
  376.5 5.3 copy-start
  385.7 2.8 copy-start.2
  385.7 2.8 copy-start.14
  388.5 4.5 copy-start.8
  393.0 6.8 %copy-start.15 = (f32[192,576]{1,0:T(8,128)}, f32[192,576]{1,0:T(8,128)S(1)}, u32[]{:S(2)}) copy-start(f32[192,576]{1,0:T(8,128)S(1)} %fusion.133) | copy-start | bytes 1327108 | tf_op jit(solution)/shard_map/while
  393.0 6.8 %copy-start.4 = (bf16[2,16,144,192]{3,2,1,0:T(8,128)(2,1)S(1)}, bf16[2,16,144,192]{3,2,1,0:T(8,128)(2,1)}, u32[]{:S(2)}) copy-start(bf16[2,16,144,192]{3,2,1,0:T(8,128)(2,1)} %copy-done.3) | copy-start | bytes 5308420 | tf_op jit(solution)/shard_map/while
  393.0 6.8 %copy-start.17 = (f32[192,192]{1,0:T(8,128)S(1)}, f32[192,192]{1,0:T(8,128)}, u32[]{:S(2)}) copy-start(f32[192,192]{1,0:T(8,128)} %get-tuple-element.310) | copy-start | bytes 442372 | tf_op jit(solution)/shard_map/while
  400.5 17.1 %copy-start.18 = (f32[192,192]{1,0:T(8,128)}, f32[192,192]{1,0:T(8,128)S(1)}, u32[]{:S(2)}) copy-start(f32[192,192]{1,0:T(8,128)S(1)} %fusion.135) | copy-start | bytes 442372 | tf_op jit(solution)/shard_map/while
  417.6 36.5 %slice-start = ((s8[4718592]{0:T(1024)(128)(4,1)}), s8[524288]{0:T(1024)(128)(4,1)S(1)}, s32[]{:S(2)}) async-start(s8[4718592]{0:T(1024)(128)(4,1)} %bitcast.188), calls=%async_computation.2 | async-start | bytes 1048576 | tf_op jit(solution)/shard_map/while
  440.8 13.3 %slice-start.1 = ((s8[4718592]{0:T(1024)(128)(4,1)}), s8[4194304]{0:T(1024)(128)(4,1)S(1)}, s32[]{:S(2)}) async-start(s8[4718592]{0:T(1024)(128)(4,1)} %bitcast.188), calls=%async_computation.3 | async-start | bytes 8388608 | tf_op jit(solution)/shard_map/while
  440.8 13.3 %copy-start.6 = (bf16[192,576]{1,0:T(8,128)(2,1)S(1)}, bf16[192,576]{1,0:T(8,128)(2,1)}, u32[]{:S(2)}) copy-start(bf16[192,576]{1,0:T(8,128)(2,1)} %get-tuple-element.329) | copy-start | bytes 663556 | tf_op jit(solution)/shard_map/while
  454.1 1.7 copy-start.12
  456.3 1.4 copy-start.13
  469.2 143.3 %all-reduce.5.cloned.1.call-start = ((), (), s32[]{:S(2)}) async-start(), calls=%async_computation | async-start | bytes 11304960 | tf_op jit(solution)/shard_map/psum | solution.py:190
  519.7 8.3 %collective-permute-start.4 = (bf16[8,3,24,192]{3,0,2,1:T(8,128)(2,1)S(1)}, bf16[8,3,24,192]{3,0,2,1:T(8,128)(2,1)S(1)}, u32[]{:S(2)}, u32[]{:S(2)}) collective-permute-start(bf16[8,3,24,192]{3,0,2,1:T(8,128)(2,1)S(1)} %slice.99), channel_id=1, source_target_pairs={{0,1},{1,2},{2,3},{4,5},{5,6},{6,7},{8,9},{9,10},{10,11},{12,13},{... | collective-permute-start | bytes 663560 | tf_op jit(solution)/shard_map/ppermute | solution.py:22
  528.1 19.4 %collective-permute-start.5 = (bf16[8,24,6,192]{3,0,2,1:T(8,128)(2,1)S(1)}, bf16[8,24,6,192]{3,0,2,1:T(8,128)(2,1)S(1)}, u32[]{:S(2)}, u32[]{:S(2)}) collective-permute-start(bf16[8,24,6,192]{3,0,2,1:T(8,128)(2,1)S(1)} %pad_maximum_fusion.7), channel_id=1, source_target_pairs={{28,0},{0,4},{4,8},{8,12},{12,16},{16,20},{20,24},{24,28},{29,1},{... | collective-permute-start | bytes 1327112 | tf_op jit(solution)/shard_map/ppermute | solution.py:16
Sparse Core Ops, SparseCore 0:
  469.3 36.3 all-reduce.6
  510.0 102.4 all-reduce.4
where the time goes:
time: 635 us; the launch traced here: 629 us
  local copies, waits for them, and re-layouts  244 us (38%)
  matrix products  161 us (25%)
  waiting for transfers between devices  110 us (17%)
  other arithmetic  79.9 us (13%)
  between operations  14.5 us (2%)
  starting transfers between devices  11.1 us (2%)
  loops' own time  9.27 us (1%)
    dot_general x4, local copies, waits for them, and re-layouts, window_backward(): jnp.dot(block_types.astype(jnp.bfloat16), bias_rows, preferred_element_ty...  64.3 us
    psum x1, waiting for transfers between devices, local(): lax.psum(totals[2].astype(jnp.bfloat16), 'lon').astype(jnp.float32)  61.7 us
    reshape x2, local copies, waits for them, and re-layouts, window_backward(): score_grad.reshape(windows, -1)  46.5 us
    mul x2, local copies, waits for them, and re-layouts, window_backward(): score_grad = attn_probs * (prob_grad - row_delta)  34.2 us
    sub x2, other arithmetic, window_backward(): exp_terms = jnp.where(allowed, jnp.exp(scores - peak_score), 0.0)  30.7 us
    dot_general x2, matrix products, window_backward(): jnp.einsum('bqhd,bkhd->bhqk', queries, key_rows, preferred_element_type=f32)  26.3 us
    dot_general x2, matrix products, window_backward(): jnp.dot(block_types.astype(jnp.bfloat16), bias_rows, preferred_element_ty...  24.7 us
    dot_general x2, matrix products, window_backward(): jnp.dot(block_types.T, score_grad.reshape(windows, -1), precision=high, p...  24.4 us
  transfers between devices with their start and end apart: 8, of which 5 were waited for; matrix products, arithmetic and copies ran while one was open for 10% of the time, Pallas kernels for 0%

commit v1 on v0

v1 whole, which is shorter than its diff:
```python
import math

import jax
import jax.numpy as jnp
from jax import lax
from jax.experimental import pallas as pl
from jax.experimental.pallas import tpu as pltpu
from jax.sharding import PartitionSpec as P

HEADS = 6
WIN_Z = 2
WIN_LAT = 6
WIN_LON = 12
WTOK = 144
ROWS_PER_GROUP = 8
GROUP = ROWS_PER_GROUP * WTOK
LOG2E = math.log2(math.e)
NT = (((1,), (1,)), ((), ()))
TN = (((0,), (0,)), ((), ()))
NN = (((1,), (0,)), ((), ()))
F32 = jnp.float32
BF16 = jnp.bfloat16


def mm(lhs, rhs, dims=NN):
    return lax.dot_general(lhs, rhs, dims, preferred_element_type=F32)


def from_behind(block, axis, distance):
    devices = range(lax.axis_size(axis))
    route = [((i - distance) % len(devices), i) for i in devices]
    return lax.ppermute(block, axis, route)


def passed_along(block, axis, distance):
    devices = range(lax.axis_size(axis))
    route = [(i - distance, i) for i in devices if i - distance in devices]
    return lax.ppermute(block, axis, route)


def kind_kernel(
    flag_ref, x0_ref, x1_ref, c0_ref, c1_ref, wq_ref, wk_ref, wv_ref, wp_ref, bias_ref,
    gx_ref, gq_ref, gk_ref, gv_ref, gp_ref, gb_ref,
    bias_rows, grad_rows,
):
    lat_step = pl.program_id(0)
    level_step = pl.program_id(1)
    first = (lat_step == 0) & (level_step == 0)
    rows = x0_ref.shape[1]
    channels = x0_ref.shape[2]
    head_dim = channels // HEADS
    breadth = rows // WIN_LAT
    tokens = WIN_Z * rows
    windows = tokens // WTOK
    scale = head_dim ** (-0.5)

    @pl.when(first)
    def _():
        gq_ref[...] = jnp.zeros_like(gq_ref)
        gk_ref[...] = jnp.zeros_like(gk_ref)
        gv_ref[...] = jnp.zeros_like(gv_ref)
        gp_ref[...] = jnp.zeros_like(gp_ref)

    def bias_group(group, carry):
        piece = bias_ref[0, :, pl.ds(pl.multiple_of(group * GROUP, GROUP), GROUP)].astype(F32) * LOG2E
        for j in range(ROWS_PER_GROUP):
            bias_rows[group * ROWS_PER_GROUP + j, 0:HEADS, 0:WTOK] = piece[:, j * WTOK : (j + 1) * WTOK]
        return carry

    lax.fori_loop(0, WTOK // ROWS_PER_GROUP, bias_group, 0)

    wrapped = level_step == pl.num_programs(1) - 1
    edge = (flag_ref[0] == 1) & (lat_step == pl.num_programs(0) - 1)
    tq = lax.broadcasted_iota(jnp.int32, (WTOK, WTOK), 0)
    tk = lax.broadcasted_iota(jnp.int32, (WTOK, WTOK), 1)
    half = WTOK // WIN_Z
    lat_half = half // 2
    zq = (tq >= half).astype(jnp.int32)
    zk = (tk >= half).astype(jnp.int32)
    yq = (tq - zq * half >= lat_half).astype(jnp.int32)
    yk = (tk - zk * half >= lat_half).astype(jnp.int32)
    bad = (zq ^ zk) * wrapped.astype(jnp.int32) + (yq ^ yk) * edge.astype(jnp.int32)
    mask = jnp.where(bad > 0, -1e30, 0.0)

    out_pos = lax.broadcasted_iota(jnp.int32, (tokens, tokens), 0)
    in_pos = lax.broadcasted_iota(jnp.int32, (tokens, tokens), 1)
    win = out_pos // WTOK
    inside = out_pos - win * WTOK
    line = inside // WIN_LON
    source = line * breadth + win * WIN_LON + (inside - line * WIN_LON)
    perm = (source == in_pos).astype(F32).astype(BF16)

    x_tok = jnp.concatenate([x0_ref[0], x1_ref[0]], axis=0)
    c_tok = jnp.concatenate([c0_ref[0], c1_ref[0]], axis=0)
    x = mm(perm, x_tok).astype(BF16)
    c = mm(perm, c_tok).astype(BF16)
    wq = wq_ref[...]
    wk = wk_ref[...]
    wv = wv_ref[...]
    q_f = mm(x, wq) * (scale * LOG2E)
    q_all = q_f.astype(BF16)
    k_all = mm(x, wk).astype(BF16)
    v_all = mm(x, wv).astype(BF16)
    mg_f = mm(c, wp_ref[...], NT)
    mg_all = mg_f.astype(BF16)

    lane = lax.broadcasted_iota(jnp.int32, (WTOK, channels), 1)
    in_head = [(lane >= h * head_dim) & (lane < (h + 1) * head_dim) for h in range(HEADS)]

    def stacked(part):
        zero = jnp.zeros_like(part)
        return jnp.concatenate([jnp.where(in_head[h], part, zero) for h in range(HEADS)], axis=0)

    mixed = []
    dq = []
    dk = []
    dv = []
    for w in range(windows):
        span = slice(w * WTOK, (w + 1) * WTOK)
        qw = q_all[span]
        kw = k_all[span]
        vw = v_all[span]
        mgw = mg_all[span]
        q_t = q_f[span].T.astype(BF16)
        mg_t = mg_f[span].T.astype(BF16)
        scores = mm(stacked(qw), kw, NT)
        prob_grads = mm(stacked(mgw), vw, NT)
        o_sum = jnp.zeros((WTOK, channels), F32)
        dq_sum = jnp.zeros((WTOK, channels), F32)
        dk_rows = []
        dv_rows = []
        for h in range(HEADS):
            hs = slice(h * WTOK, (h + 1) * WTOK)
            cs = slice(h * head_dim, (h + 1) * head_dim)
            t = scores[hs] + (bias_rows[:, h, :][:, :WTOK] + mask)
            e = jnp.exp2(t - jnp.max(t, axis=1, keepdims=True))
            p = e * (1.0 / jnp.sum(e, axis=1, keepdims=True))
            pb = p.astype(BF16)
            pdp = p * prob_grads[hs]
            ds = pdp - p * jnp.sum(pdp, axis=1, keepdims=True)
            dsb = ds.astype(BF16)
            if w == 0:
                grad_rows[:, h, 0:WTOK] = ds
            else:
                grad_rows[:, h, 0:WTOK] = grad_rows[:, h, 0:WTOK] + ds
            o_sum = jnp.where(in_head[h], mm(pb, vw), o_sum)
            dq_sum = jnp.where(in_head[h], mm(dsb, kw), dq_sum)
            dv_rows.append(mm(mg_t[cs], pb))
            dk_rows.append(mm(q_t[cs], dsb))
        mixed.append(o_sum)
        dq.append(dq_sum * scale)
        dk.append(jnp.concatenate(dk_rows, axis=0).T * (1.0 / LOG2E))
        dv.append(jnp.concatenate(dv_rows, axis=0).T)
    mixed = jnp.concatenate(mixed, axis=0).astype(BF16)
    dq = jnp.concatenate(dq, axis=0).astype(BF16)
    dk = jnp.concatenate(dk, axis=0).astype(BF16)
    dv = jnp.concatenate(dv, axis=0).astype(BF16)
    gp_ref[...] += mm(mixed, c, TN)
    gq_ref[...] += mm(x, dq, TN)
    gk_ref[...] += mm(x, dk, TN)
    gv_ref[...] += mm(x, dv, TN)
    gx = (mm(dq, wq, NT) + mm(dk, wk, NT) + mm(dv, wv, NT)).astype(BF16)
    gx = mm(perm, gx, TN).astype(BF16)
    for z in range(WIN_Z):
        gx_ref[z] = gx[z * rows : (z + 1) * rows]

    def grad_group(group, carry):
        pieces = [
            grad_rows[group * ROWS_PER_GROUP + j, 0:HEADS, 0:WTOK] for j in range(ROWS_PER_GROUP)
        ]
        joined = jnp.concatenate(pieces, axis=1).astype(BF16)
        gb_ref[0, :, pl.ds(pl.multiple_of(group * GROUP, GROUP), GROUP)] = joined
        return carry

    lax.fori_loop(0, WTOK // ROWS_PER_GROUP, grad_group, 0)


def kinds_backward(flag, frame_in, frame_cot, weights, weight_proj, bias_table, lat_range):
    levels, cells, channels = frame_in.shape
    types, heads, pairs = bias_table.shape
    level_windows = levels // WIN_Z
    lat_windows = types // level_windows
    first, last = lat_range
    rows = cells // lat_windows
    count = last - first

    def level_block(offset):
        return pl.BlockSpec(
            (1, rows, channels),
            lambda b, a, *_: ((WIN_Z * a + offset) % levels, b + first, 0),
        )

    def whole(shape):
        return pl.BlockSpec(shape, lambda b, a, *_: (0, 0))

    square = whole((channels, channels))
    x_specs = [level_block(1), level_block(2)]
    f32_square = jax.ShapeDtypeStruct((channels, channels), F32)
    return pl.pallas_call(
        kind_kernel,
        grid_spec=pltpu.PrefetchScalarGridSpec(
            num_scalar_prefetch=1,
            grid=(count, level_windows),
            in_specs=x_specs + x_specs + [square] * 4
            + [
                pl.BlockSpec(
                    (1, heads, pairs), lambda b, a, *_: ((b + first) * level_windows + a, 0, 0)
                )
            ],
            out_specs=[
                pl.BlockSpec((WIN_Z, rows, channels), lambda b, a, *_: (a, b, 0)),
                square, square, square, square,
                pl.BlockSpec((1, heads, pairs), lambda b, a, *_: (b * level_windows + a, 0, 0)),
            ],
            scratch_shapes=[
                pltpu.VMEM((WTOK, 8, 256), F32),
                pltpu.VMEM((WTOK, 8, 256), F32),
            ],
        ),
        out_shape=[
            jax.ShapeDtypeStruct((levels, count * rows, channels), BF16),
            f32_square, f32_square, f32_square, f32_square,
            jax.ShapeDtypeStruct((count * level_windows, heads, pairs), BF16),
        ],
        compiler_params=pltpu.CompilerParams(
            dimension_semantics=("arbitrary", "arbitrary"), vmem_limit_bytes=56 * 1024 * 1024
        ),
    )(flag, frame_in, frame_in, frame_cot, frame_cot, *weights, weight_proj, bias_table)


def local(normed, cotangent, weight_qkv, weight_proj, bias_table):
    levels, height, breadth, channels = normed.shape
    level_shift = WIN_Z // 2
    lat_shift = WIN_LAT // 2
    lon_shift = WIN_LON // 2
    across = from_behind((normed[:, :, :lon_shift], cotangent[:, :, :lon_shift]), "lon", -1)
    wide_in = jnp.concatenate([normed[:, :, lon_shift:], across[0]], axis=2)
    wide_cot = jnp.concatenate([cotangent[:, :, lon_shift:], across[1]], axis=2)
    upward = passed_along((wide_in[:, :lat_shift], wide_cot[:, :lat_shift]), "lat", -1)
    frame_in = jnp.concatenate([wide_in[:, lat_shift:], upward[0]], axis=1)
    frame_cot = jnp.concatenate([wide_cot[:, lat_shift:], upward[1]], axis=1)
    flag = (lax.axis_index("lat") == lax.axis_size("lat") - 1).astype(jnp.int32).reshape(1)
    lat_windows = height // WIN_LAT
    weights = tuple(weight_qkv[:, i * channels : (i + 1) * channels] for i in range(3))
    frame_in = frame_in.reshape(levels, height * breadth, channels)
    frame_cot = frame_cot.reshape(levels, height * breadth, channels)
    framed_grad, gq, gk, gv, gp, gb = kinds_backward(
        flag, frame_in, frame_cot, weights, weight_proj, bias_table, (0, lat_windows)
    )
    framed_grad = framed_grad.reshape(levels, height, breadth, channels)
    returned = passed_along(framed_grad[:, height - lat_shift :], "lat", 1)
    wide_grad = jnp.concatenate([returned, framed_grad[:, : height - lat_shift]], axis=1)
    sideways = from_behind(wide_grad[:, :, breadth - lon_shift :], "lon", 1)
    shifted_grad = jnp.concatenate([sideways, wide_grad[:, :, : breadth - lon_shift]], axis=2)
    input_grad = jnp.roll(shifted_grad, level_shift, axis=0)
    small = jnp.concatenate([gq, gk, gv, gp], axis=1).astype(BF16)
    small = lax.psum(small, ("lat", "lon")).astype(F32)
    bias_grad = lax.psum(gb, "lon").astype(F32)
    return (input_grad, small[:, : 3 * channels], small[:, 3 * channels :], bias_grad)


def solution(mesh):
    in_specs = (
        P(None, "lat", "lon", None),
        P(None, "lat", "lon", None),
        P(),
        P(),
        P("lat", None, None),
    )
    out_specs = (P(None, "lat", "lon", None), P(), P(), P("lat", None, None))
    return jax.shard_map(local, mesh=mesh, in_specs=in_specs, out_specs=out_specs, check_vma=False)
```

time: 635 us -> 407 us (0.64)
  local copies, waits for them, and re-layouts: 244 us -> 28.1 us
  matrix products: 161 us -> 0 us
  Pallas kernels: 0 us -> 120 us
  waiting for transfers between devices: 110 us -> 221 us
  other arithmetic: 79.9 us -> 12.3 us
  loops' own time: 9.27 us -> 0 us
    dot_general x26 -> x0, matrix products: 161 us -> none  [the longest x2 26.3 us: window_backward(): jnp.einsum('bqhd,bkhd->bhqk', queries, key_rows, preferred_element_type=f32)]
    psum x2, waiting for transfers between devices: 83.6 us -> 206 us  [the longest x1 114 us: local(): small = lax.psum(small, ('lat', 'lon')).astype(F32)]
    pallas_call x0 -> x1, Pallas kernels: none -> 120 us  [kinds_backward(): pl.pallas_call(kind_kernel, grid_spec=pltpu.PrefetchScalarGridSpec(num_sc...]
    reshape x7 -> x0, local copies, waits for them, and re-layouts: 70.1 us -> none  [the longest x2 46.5 us: window_backward(): score_grad.reshape(windows, -1)]
    dot_general x4 -> x0, local copies, waits for them, and re-layouts: 64.3 us -> none  [window_backward(): jnp.dot(block_types.astype(jnp.bfloat16), bias_rows, preferred_element_ty...]
    mul x2 -> x0, local copies, waits for them, and re-layouts: 34.2 us -> none  [window_backward(): score_grad = attn_probs * (prob_grad - row_delta)]
    sub x2 -> x0, other arithmetic: 30.7 us -> none  [window_backward(): exp_terms = jnp.where(allowed, jnp.exp(scores - peak_score), 0.0)]
    mul x3 -> x0, other arithmetic: 20.2 us -> none  [the longest x2 20.2 us: window_backward(): score_grad = attn_probs * (prob_grad - row_delta)]
  transfers between devices with their start and end apart: 8 -> 8, of which waited for: 5 -> 5; matrix products, arithmetic and copies ran while one was open for 10% -> 6% of each run, Pallas kernels for 0% -> 0%
where the time goes in v1:
time: 407 us; the launch traced here: 406 us
  waiting for transfers between devices  221 us (54%)
  Pallas kernels  120 us (29%)
  local copies, waits for them, and re-layouts  28.1 us (7%)
  between operations  14.2 us (3%)
  other arithmetic  12.3 us (3%)
  starting transfers between devices  10.4 us (3%)
    pallas_call x1, Pallas kernels, kinds_backward(): pl.pallas_call(kind_kernel, grid_spec=pltpu.PrefetchScalarGridSpec(num_sc...  120 us
    psum x1, waiting for transfers between devices, local(): small = lax.psum(small, ('lat', 'lon')).astype(F32)  114 us
    psum x1, waiting for transfers between devices, local(): bias_grad = lax.psum(gb, 'lon').astype(F32)  91.8 us
    ppermute x3, waiting for transfers between devices, passed_along(): return lax.ppermute(block, axis, route)  14.6 us
    unnamed x12, local copies, waits for them, and re-layouts  14.3 us
  transfers between devices with their start and end apart: 8, of which 5 were waited for; matrix products, arithmetic and copies ran while one was open for 6% of the time, Pallas kernels for 0%

profile of v1, /device:TPU:0, one launch (start us, length us, event | category | flops | bytes accessed | tf_op | source)
XLA Modules:
  0.0 406.4 jit_solution(12479650603231368200)
XLA Ops:
  7.2 0.0 slice-start
  7.2 0.0 all-reduce.3.cloned.1.call-start
  7.2 1.3 slice.60
  8.5 0.0 copy-start.1
  8.5 0.9 copy.28
  9.4 3.4 collective-permute-start
  12.8 0.0 slice-done
  12.8 1.0 copy.29
  13.7 0.7 collective-permute-start.2
  14.4 0.0 copy-done.1
  14.4 0.0 copy-start.2
  14.4 2.7 slice.59
  17.1 0.0 copy-done.2
  17.1 1.3 slice.63
  18.5 0.0 copy-start.3
  18.5 0.0 copy-start
  18.5 5.9 %copy.24.bias_ref = bf16[16,6,20736]{2,1,0:T(8,128)(2,1)} copy(bf16[16,6,20736]{2,0,1:T(8,128)(2,1)} %param.9) | data formatting | bytes 7962624 | tf_op args[4]
  24.3 0.0 copy-done.3
  24.4 0.8 fusion.3
  25.1 0.0 collective-permute-done
  25.1 1.2 copy.21
  26.4 0.0 copy-done
  26.4 0.1 pad_maximum_fusion.8
  26.5 1.3 collective-permute-start.1
  27.8 0.8 fusion.2
  28.6 0.0 collective-permute-done.2
  28.6 0.2 copy.23
  28.7 0.1 pad_maximum_fusion.7
  28.8 1.5 collective-permute-start.3
  30.3 0.8 fusion.1
  31.1 7.2 %collective-permute-done.1 = bf16[8,3,24,192]{3,2,1,0:T(8,128)(2,1)S(1)} collective-permute-done((bf16[8,3,24,192]{3,2,1,0:T(8,128)(2,1)S(1)}, bf16[8,3,24,192]{3,2,1,0:T(8,128)(2,1)S(1)}, u32[]{:S(2)}, u32[]{:S(2)}) %collective-permute-start.1) | collective-permute-done | bytes 221216 | tf_op jit(solution)/shard_map/ppermute | solution.py:38
  38.2 1.8 pad_maximum_fusion.4
  40.0 3.4 collective-permute-done.3
  43.4 1.8 pad_maximum_fusion.5
  45.2 120.1 %shard_map.84 = (bf16[8,576,192]{2,1,0:T(8,128)(2,1)}, f32[192,192]{1,0:T(8,128)}, f32[192,192]{1,0:T(8,128)}, f32[192,192]{1,0:T(8,128)}, f32[192,192]{1,0:T(8,128)}, /*index=5*/bf16[16,6,20736]{2,1,0:T(8,128)(2,1)}) custom-call(s32[1]{0:T(128)} %bitcast.flag_ref, bf16[8,576,192]{2,1,0:T(8,128)(2,1)} %bitcast.4, bf16[8,576,192]{2,1,0:T(8,128)(2,1)} %bitcast.5, ...), custom_call_target="tpu_custom_call" | custom-call | tf_op jit(solution)/shard_map/pallas_call | solution.py:199
  165.4 0.9 convert.13
  166.3 0.9 convert.14
  167.3 0.9 convert.15
  168.2 0.9 convert.16
  169.1 0.9 pad_maximum_fusion.9
  170.0 0.0 all-reduce.3.cloned.1.call-update
  170.0 0.0 all-reduce.5.cloned.1.call-start
  170.1 0.7 all-reduce.5.cloned.1.call-update
  170.8 1.0 slice.82
  171.8 3.5 collective-permute-start.4
  175.3 1.7 slice.83
  177.0 4.0 collective-permute-done.4
  181.0 0.2 pad_maximum_fusion.6
  181.3 0.1 copy.25
  181.4 0.1 collective-permute-start.5
  181.4 114.1 %all-reduce.3.cloned.1.call-done = bf16[192,768]{1,0:T(8,128)(2,1)} async-done(((bf16[192,768]{1,0:T(8,128)(2,1)}), bf16[192,768]{1,0:T(8,128)(2,1)}) %all-reduce.3.cloned.1.call-update) | async-done | bytes 294928 | tf_op jit(solution)/shard_map/psum | solution.py:257
  295.5 1.7 slice.85
  297.2 1.8 slice.84
  298.9 0.0 collective-permute-done.5
  298.9 0.2 copy.26
  299.1 2.2 fusion
  301.3 91.8 %all-reduce.5.cloned.1.call-done = bf16[16,6,20736]{2,1,0:T(8,128)(2,1)} async-done(((bf16[16,6,20736]{2,1,0:T(8,128)(2,1)}), bf16[16,6,20736]{2,1,0:T(8,128)(2,1)}) %all-reduce.5.cloned.1.call-update) | async-done | bytes 3981328 | tf_op jit(solution)/shard_map/psum | solution.py:258
  393.1 6.5 %copy.27 = f32[16,6,20736]{2,0,1:T(8,128)} copy(bf16[16,6,20736]{2,1,0:T(8,128)(2,1)} %all-reduce.5.cloned.1.call-done) | data formatting | bytes 11943936
Async XLA Ops:
  7.2 5.6 %slice-start = ((bf16[8,24,24,192]{3,2,1,0:T(8,128)(2,1)}), bf16[8,24,6,192]{3,2,1,0:T(8,128)(2,1)S(1)}, s32[]{:S(2)}) async-start(bf16[8,24,24,192]{3,2,1,0:T(8,128)(2,1)} %param.6), calls=%async_computation.2 | async-start | bytes 1572864 | tf_op jit(solution)/shard_map/slice | solution.py:236
  7.2 288.3 %all-reduce.3.cloned.1.call-start = ((), (), s32[]{:S(2)}) async-start(), calls=%async_computation | async-start | bytes 589824 | tf_op jit(solution)/shard_map/psum | solution.py:257
  8.5 5.9 %copy-start.1 = (bf16[8,24,24,192]{3,2,1,0:T(8,128)(2,1)S(1)}, bf16[8,24,24,192]{3,2,1,0:T(8,128)(2,1)}, u32[]{:S(2)}) copy-start(bf16[8,24,24,192]{3,2,1,0:T(8,128)(2,1)} %param.5) | copy-start | bytes 5308420
  9.4 15.7 %collective-permute-start = (bf16[8,24,6,192]{3,1,2,0:T(8,128)(2,1)}, bf16[8,24,6,192]{3,1,2,0:T(8,128)(2,1)}, u32[]{:S(2)}, u32[]{:S(2)}) collective-permute-start(bf16[8,24,6,192]{3,1,2,0:T(8,128)(2,1)} %copy.28), channel_id=1, source_target_pairs={{4,0},{8,4},{12,8},{16,12},{20,16},{24,20},{28,24},{0,28},{5,1},{9... | collective-permute-start | bytes 1327112 | tf_op jit(solution)/shard_map/ppermute | solution.py:32
  13.7 14.8 %collective-permute-start.2 = (bf16[8,24,6,192]{3,1,2,0:T(8,128)(2,1)}, bf16[8,24,6,192]{3,1,2,0:T(8,128)(2,1)S(1)}, u32[]{:S(2)}, u32[]{:S(2)}) collective-permute-start(bf16[8,24,6,192]{3,1,2,0:T(8,128)(2,1)} %copy.29), channel_id=1, source_target_pairs={{4,0},{8,4},{12,8},{16,12},{20,16},{24,20},{28,24},{0,28},{5,1},{9... | collective-permute-start | bytes 1327112 | tf_op jit(solution)/shard_map/ppermute | solution.py:32
  14.4 2.7 copy-start.2
  18.5 5.9 %copy-start.3 = (bf16[192,576]{1,0:T(8,128)(2,1)S(1)}, bf16[192,576]{1,0:T(8,128)(2,1)}, u32[]{:S(2)}) copy-start(bf16[192,576]{1,0:T(8,128)(2,1)} %param.7) | copy-start | bytes 663556
  18.5 7.9 %copy-start = (bf16[8,24,18,192]{3,2,1,0:T(8,128)(2,1)S(1)}, bf16[8,24,18,192]{3,2,1,0:T(8,128)(2,1)}, u32[]{:S(2)}) copy-start(bf16[8,24,18,192]{3,2,1,0:T(8,128)(2,1)} %slice.59) | copy-start | bytes 3981316
  26.5 11.8 %collective-permute-start.1 = (bf16[8,3,24,192]{3,2,1,0:T(8,128)(2,1)S(1)}, bf16[8,3,24,192]{3,2,1,0:T(8,128)(2,1)S(1)}, u32[]{:S(2)}, u32[]{:S(2)}) collective-permute-start(bf16[8,3,24,192]{3,2,1,0:T(8,128)(2,1)S(1)} %pad_maximum_fusion.8), channel_id=1, source_target_pairs={{1,0},{2,1},{3,2},{5,4},{6,5},{7,6},{9,8},{10,9},{11,10},{13,12},{... | collective-permute-start | bytes 663560 | tf_op jit(solution)/shard_map/ppermute | solution.py:38
  28.8 14.6 %collective-permute-start.3 = (bf16[8,3,24,192]{3,2,1,0:T(8,128)(2,1)S(1)}, bf16[8,3,24,192]{3,2,1,0:T(8,128)(2,1)S(1)}, u32[]{:S(2)}, u32[]{:S(2)}) collective-permute-start(bf16[8,3,24,192]{3,2,1,0:T(8,128)(2,1)S(1)} %pad_maximum_fusion.7), channel_id=1, source_target_pairs={{1,0},{2,1},{3,2},{5,4},{6,5},{7,6},{9,8},{10,9},{11,10},{13,12},{... | collective-permute-start | bytes 663560 | tf_op jit(solution)/shard_map/ppermute | solution.py:38
  170.0 223.0 %all-reduce.5.cloned.1.call-start = ((), (), s32[]{:S(2)}) async-start(), calls=%async_computation.1 | async-start | bytes 10616832 | tf_op jit(solution)/shard_map/psum | solution.py:258
  171.8 9.3 %collective-permute-start.4 = (bf16[8,3,24,192]{3,2,1,0:T(8,128)(2,1)S(1)}, bf16[8,3,24,192]{3,2,1,0:T(8,128)(2,1)S(1)}, u32[]{:S(2)}, u32[]{:S(2)}) collective-permute-start(bf16[8,3,24,192]{3,2,1,0:T(8,128)(2,1)S(1)} %slice.82), channel_id=1, source_target_pairs={{0,1},{1,2},{2,3},{4,5},{5,6},{6,7},{8,9},{9,10},{10,11},{12,13},{... | collective-permute-start | bytes 663560 | tf_op jit(solution)/shard_map/ppermute | solution.py:38
  181.4 117.6 %collective-permute-start.5 = (bf16[8,24,6,192]{3,1,2,0:T(8,128)(2,1)S(1)}, bf16[8,24,6,192]{3,1,2,0:T(8,128)(2,1)S(1)}, u32[]{:S(2)}, u32[]{:S(2)}) collective-permute-start(bf16[8,24,6,192]{3,1,2,0:T(8,128)(2,1)S(1)} %copy.25), channel_id=1, source_target_pairs={{28,0},{0,4},{4,8},{8,12},{12,16},{16,20},{20,24},{24,28},{29,1},{... | collective-permute-start | bytes 1327112 | tf_op jit(solution)/shard_map/ppermute | solution.py:32
Sparse Core Ops, SparseCore 0:
  170.1 125.3 all-reduce.2
  298.8 94.2 all-reduce.4
